TPU v7x, 32 devices: a whole 2x2x4 slice. The times are simulated.
32 devices in a mesh: grp: 2 (over y), lon: 16 (over z, x, core), lat: 1.
Axes of the slice: x: 2, y: 2, z: 4, core: 2. Of those that a mesh axis runs over, the one named last changes fastest.
Arguments:
- surface_field: bfloat16 [256, 128, 256], P(('grp', 'lat'), 'lon'), parts along dimension 0, may hold values from -6 to 6
- conv_a: bfloat16 [3, 3, 256, 512], replicated, may hold values from -0.125 to 0.125
- conv_b: bfloat16 [3, 3, 512, 512], replicated, may hold values from -0.09375 to 0.09375
- norm_gain: float32 [512], replicated, may hold values from 0.1 to 1.9
- qkv_weight: bfloat16 [512, 3072], replicated, may hold values from -3 to 3, as said below
- out_weight: bfloat16 [1024, 512], replicated, may hold values from -0.1875 to 0.1875
Outputs:
- mixed_out: bfloat16 [64, 32, 512], P(('grp', 'lat'), 'lon'), parts along dimension 0
There are 2 independent parts, one for each index of `grp`. A program takes and returns all parts, laid end to end along the dimension named above; an argument that names none is the same for every part. Nothing has to cross between parts.
Inputs may be any that keep to these rules, and one draw needn't show every extreme that they name: `qkv_weight`: columns hold queries, keys and values in that order, each 16 heads of 64 entries.
All inputs are finite; a program needn't handle non-finite values.
Results may differ from a plain program's by a relative error of at most 0.012.
The roundings to bfloat16 on the way count: a program that leaves them out, or rounds other values in their place, can miss the bound.
Values may be sent and summed in bfloat16 or wider, within the bound.
A program may use at most 128 MiB of HBM per device.

v0:
```python
import functools

import jax
import jax.numpy as jnp
from jax import lax
from jax.experimental import pallas as pl
from jax.experimental.pallas import tpu as pltpu
from jax.sharding import PartitionSpec as P

CB = 512
HEADS = 16
HEAD_DIM = 64
CHUNKS = 2


def with_halo(block, sides, width):
    for axis, dim in sides:
        count = lax.axis_size(axis)
        forward = [(i, i + 1) for i in range(count - 1)]
        forward.append((count - 1, 0))
        backward = [(target, source) for source, target in forward]
        low = lax.ppermute(
            lax.slice_in_dim(block, block.shape[dim] - width, None, axis=dim), axis, forward
        )
        high = lax.ppermute(lax.slice_in_dim(block, 0, width, axis=dim), axis, backward)
        block = jnp.concatenate([low, block, high], axis=dim)
    return block


def partner_2(value, axis, distance):
    mask = 2**distance
    pairs = [(source, source ^ mask) for source in range(lax.axis_size(axis))]
    return lax.ppermute(value, axis, pairs)


def convolve(values_in, weight):
    return lax.conv_general_dilated(
        values_in[None],
        weight,
        (1, 1),
        "VALID",
        dimension_numbers=("NHWC", "HWIO", "NHWC"),
        preferred_element_type=jnp.float32,
    )[0]


def average_pool(values_in):
    rows_in, cols_in, chans_in = values_in.shape
    return values_in.reshape(rows_in // 2, 2, cols_in // 2, 2, chans_in).mean(axis=(1, 3))


def layer_norm(tokens_flat, norm_gain):
    centred = tokens_flat - jnp.mean(tokens_flat, axis=-1, keepdims=True)
    spread = jnp.mean(centred * centred, axis=-1, keepdims=True)
    return centred * lax.rsqrt(spread + 0.01) * norm_gain


def softmax_rows(scores):
    maxima = jnp.max(scores, axis=-1, keepdims=True)
    raised = jnp.exp(scores - maxima)
    return raised / jnp.sum(raised, axis=-1, keepdims=True)


def keep_rows(values_in, rows_here, lat_count, lat_where, margin):
    first_row = lat_where * rows_here - margin
    rowpos = first_row + jnp.arange(values_in.shape[0], dtype=jnp.int32)
    inside = (rowpos >= 0) & (rowpos < rows_here * lat_count)
    return jnp.where(inside[:, None, None], values_in, jnp.zeros((), values_in.dtype))


def body(surface_field, conv_a, conv_b, norm_gain, qkv_weight, out_weight):
    lon_count = lax.axis_size("lon")
    lat_count = lax.axis_size("lat")
    lat_where = lax.axis_index("lat")
    rows_here = surface_field.shape[0]
    padded_field = with_halo(surface_field, (("lon", 1), ("lat", 0)), 1)
    padded_field = keep_rows(padded_field, rows_here, lat_count, lat_where, 1)
    first_out = jax.nn.silu(convolve(padded_field, conv_a))
    pooled_first = average_pool(first_out).astype(jnp.bfloat16)
    ready_rows = with_halo(pooled_first, (("lon", 1), ("lat", 0)), 1)
    ready_rows = keep_rows(ready_rows, rows_here // 2, lat_count, lat_where, 1)
    second_out = jax.nn.silu(convolve(ready_rows, conv_b))
    pooled_second = average_pool(second_out)
    tok_rows, tok_cols = (pooled_second.shape[0], pooled_second.shape[1])
    local_tokens = tok_rows * tok_cols
    tokens_flat = pooled_second.reshape(local_tokens, CB)
    normed = layer_norm(tokens_flat, norm_gain).astype(jnp.bfloat16)
    projected = jnp.dot(normed, qkv_weight, preferred_element_type=jnp.float32).astype(jnp.bfloat16)
    residues = max(1, lon_count // HEADS)
    groups = lon_count // residues
    per_slot = HEADS // groups
    per_residue = local_tokens // residues
    arranged = projected.reshape(per_residue, residues, 3, groups, per_slot, HEAD_DIM)
    outgoing = arranged.transpose(2, 1, 3, 4, 0, 5).reshape(
        3, lon_count, per_slot, per_residue, HEAD_DIM
    )
    swap_bits = list(range(groups.bit_length() - 1, lon_count.bit_length() - 1))
    arrived = lax.all_to_all(outgoing, "lon", split_axis=1, concat_axis=3, tiled=True)
    queries = arrived[0, 0]
    keys_vals = arrived[1:, 0]
    for bit_pos in swap_bits:
        partner = partner_2(keys_vals, "lon", bit_pos)
        keys_vals = jnp.concatenate([keys_vals, partner], axis=2)
    for bit_pos in range(lat_count.bit_length() - 1):
        partner = partner_2(keys_vals, "lat", bit_pos)
        keys_vals = jnp.concatenate([keys_vals, partner], axis=2)
    score_scale = HEAD_DIM ** (-0.5)
    scores = (
        jnp.einsum("hqd,hkd->hqk", queries, keys_vals[0], preferred_element_type=jnp.float32)
        * score_scale
    )
    weights = softmax_rows(scores).astype(jnp.bfloat16)
    head_out = jnp.einsum(
        "hqk,hkd->hqd", weights, keys_vals[1], preferred_element_type=jnp.float32
    ).astype(jnp.bfloat16)
    returned = lax.all_to_all(head_out[None], "lon", split_axis=2, concat_axis=0, tiled=True)
    attended = returned.reshape(residues, groups, per_slot, per_residue, HEAD_DIM).transpose(
        3, 0, 1, 2, 4
    )
    attended = attended.reshape(local_tokens, HEADS * HEAD_DIM)
    mixed_out = tokens_flat + jnp.dot(attended, out_weight, preferred_element_type=jnp.float32)
    return mixed_out.reshape(tok_rows, tok_cols, CB).astype(jnp.bfloat16)


def roll_rows(values, amount):
    count = values.shape[0]
    moved = pltpu.roll(values, amount % count, 0)
    rowpos = lax.broadcasted_iota(jnp.int32, values.shape, 0)
    edge = 0 if amount == 1 else count - 1
    return jnp.where(rowpos == edge, jnp.zeros_like(moved), moved)


def silu(v):
    return v / (1.0 + jnp.exp(-v))


def fused_kernel(
    n, cols, toks, heads, hdim,
    x_hbm, wa_hbm, wb_hbm, gain_ref, wqkv_hbm, wo_hbm, out_ref,
    x_v, wa, wb, wqkv, wo, xf, xs, edge_out, edge_in, ps, pedge_out, pedge_in,
    gat, keys, vals, qmask, att,
    load_sem, halo_send, halo_recv, z_send, far_send, x_send, c_send, recv,
):
    width = heads * hdim
    me = lax.axis_index("lon")
    core, x_at, z_at = me % 2, (me // 2) % 2, me // 4
    zn = n // 4
    left, right = (me + n - 1) % n, (me + 1) % n
    other_core = me + 1 - 2 * core
    other_x = me + 2 - 4 * x_at
    has_up, has_dn = z_at < zn - 1, z_at > 0

    loads = [
        pltpu.make_async_copy(s, d, load_sem.at[i])
        for i, (s, d) in enumerate(
            ((x_hbm, x_v), (wa_hbm, wa), (wb_hbm, wb), (wqkv_hbm, wqkv), (wo_hbm, wo))
        )
    ]
    for c in loads:
        c.start()

    barrier = pltpu.get_barrier_semaphore()

    def greet(dev):
        pl.semaphore_signal(barrier, inc=1, device_id={"lon": dev})

    for dev in (left, right, other_core, other_x):
        greet(dev)

    @pl.when(has_up)
    def _():
        greet(me + 4)

    @pl.when(has_dn)
    def _():
        greet(me - 4)

    ends = jnp.where(has_up, 1, 0) + jnp.where(has_dn, 1, 0)
    for d in range(3, zn):
        far_up, far_dn = z_at + d < zn, z_at - d >= 0
        ends = ends + jnp.where(far_up, 1, 0) + jnp.where(far_dn, 1, 0)

        @pl.when(far_up)
        def _(d=d):
            greet(me + 4 * d)

        @pl.when(far_dn)
        def _(d=d):
            greet(me - 4 * d)

    loads[0].wait()
    srows = x_v.shape[0] // cols // 4
    step = 4 * cols
    halves = xf.shape[0]
    for h in range(halves):
        lanes = slice(128 * h, 128 * h + 128)
        xf[h, 0:cols, :] = jnp.zeros((cols, 128), jnp.float32)
        xf[h, cols + x_v.shape[0] :, :] = jnp.zeros((cols, 128), jnp.float32)
        xf[h, cols : cols + x_v.shape[0], :] = x_v[:, lanes].astype(jnp.float32)

    def pick(k, j):
        parts = [
            xf[h, pl.ds(cols + k * cols + j, srows, stride=step), :] for h in range(halves)
        ]
        return jnp.concatenate(parts, axis=1).astype(jnp.bfloat16)

    for side, j in ((0, 0), (1, cols - 1)):
        for k in range(4):
            edge_out[side, k] = pick(k, j)
    pl.semaphore_wait(barrier, 4 + ends)

    def halo(level, src, dst):
        return [
            pltpu.make_async_remote_copy(
                src_ref=src.at[side],
                dst_ref=dst.at[1 - side],
                send_sem=halo_send.at[2 * level + side],
                recv_sem=halo_recv.at[2 * level + 1 - side],
                device_id={"lon": dev},
            )
            for side, dev in ((0, left), (1, right))
        ]

    first = halo(0, edge_out, edge_in)
    for c in first:
        c.start()
    for j in range(cols):
        for k in range(-1, 5):
            xs[k + 1, j + 1] = pick(k, j)

    pcols = cols // 2

    def conv_first(jp):
        taps = [
            xs[a : a + 4, 2 * jp + b : 2 * jp + b + 2].reshape(8 * srows, xs.shape[-1])
            for a in range(3)
            for b in range(3)
        ]
        y = silu(
            jnp.dot(jnp.concatenate(taps, axis=1), wa[...], preferred_element_type=jnp.float32)
        )
        y = y.reshape(4, 2, srows, y.shape[-1])
        even = (y[0, 0] + y[0, 1] + y[1, 0] + y[1, 1]) * 0.25
        odd = (y[2, 0] + y[2, 1] + y[3, 0] + y[3, 1]) * 0.25
        return even, odd

    def put_pooled(at, even, odd):
        ps[0, at] = roll_rows(odd, 1).astype(jnp.bfloat16)
        ps[1, at] = even.astype(jnp.bfloat16)
        ps[2, at] = odd.astype(jnp.bfloat16)
        ps[3, at] = roll_rows(even, -1).astype(jnp.bfloat16)

    loads[1].wait()
    for jp in range(1, pcols - 1):
        put_pooled(jp + 1, *conv_first(jp))

    for c in first:
        c.wait()
    for side, at in ((0, 0), (1, cols + 1)):
        for k in range(4):
            xs[k + 1, at] = edge_in[side, k]
        xs[0, at] = roll_rows(edge_in[side, 3].astype(jnp.float32), 1).astype(jnp.bfloat16)
        xs[5, at] = roll_rows(edge_in[side, 0].astype(jnp.float32), -1).astype(jnp.bfloat16)
    second = halo(1, pedge_out, pedge_in)
    for side, jp in ((0, 0), (1, pcols - 1)):
        even, odd = conv_first(jp)
        pedge_out[side, 0] = even.astype(jnp.bfloat16)
        pedge_out[side, 1] = odd.astype(jnp.bfloat16)
        put_pooled(jp + 1, even, odd)
        second[side].start()

    def conv_second(pieces):
        z = silu(jnp.dot(pieces, wb[...], preferred_element_type=jnp.float32))
        return z.reshape(2, 2, srows, z.shape[-1])

    loads[2].wait()
    chans = ps.shape[-1]
    inner = conv_second(
        jnp.concatenate(
            [
                ps[a : a + 2, 1 + b : 3 + b].reshape(4 * srows, chans)
                for a in range(3)
                for b in range(3)
            ],
            axis=1,
        )
    )
    for c in second:
        c.wait()
    for side, at in ((0, 0), (1, pcols + 1)):
        put_pooled(
            at,
            pedge_in[side, 0].astype(jnp.float32),
            pedge_in[side, 1].astype(jnp.float32),
        )
    outer = conv_second(
        jnp.concatenate(
            [
                jnp.concatenate(
                    [
                        ps[a : a + 2, b].reshape(2 * srows, chans),
                        ps[a : a + 2, pcols - 1 + b].reshape(2 * srows, chans),
                    ],
                    axis=0,
                )
                for a in range(3)
                for b in range(3)
            ],
            axis=1,
        )
    )
    tokens = jnp.concatenate(
        [
            (inner[0, side] + inner[1, side] + outer[side, 0] + outer[side, 1]) * 0.25
            for side in range(2)
        ],
        axis=0,
    )
    centred = tokens - jnp.mean(tokens, axis=-1, keepdims=True)
    spread = jnp.mean(centred * centred, axis=-1, keepdims=True)
    normed = (centred * lax.rsqrt(spread + 0.01) * gain_ref[...]).astype(jnp.bfloat16)
    chunks = gat.shape[1]
    gat[me] = normed.reshape(gat.shape[1:])
    sent = []

    def go(cond, *made):
        copy = functools.partial(*made)
        sent.append((cond, copy))
        if cond is None:
            copy().start()
        else:
            pl.when(cond)(lambda: copy().start())

    def send(block, ch, dev, sem):
        return pltpu.make_async_remote_copy(
            src_ref=gat.at[block, ch],
            dst_ref=gat.at[block, ch],
            send_sem=sem,
            recv_sem=recv.at[block, ch],
            device_id={"lon": dev},
        )

    def along(block, ch, sign):
        return send(block, ch, me + 4 * sign, z_send.at[(1 - sign) // 2, block // 4, ch])

    def far(block, ch, sign, d):
        return send(block, ch, me + 4 * sign * d, far_send.at[(1 - sign) // 2, d, ch])

    def across(block, ch):
        return send(block, ch, other_x, x_send.at[block // 4, ch])

    def beside(block, ch):
        return send(block, ch, other_core, c_send.at[block // 2, ch])

    def arrived(block, ch):
        send(block, ch, other_core, c_send.at[0, 0]).wait_recv()

    def rows_at(d):
        if d == 0:
            return [(0, None, z_at)]
        return [
            (sign, (z_at + sign * d >= 0) & (z_at + sign * d < zn), z_at + sign * d)
            for sign in (-1, 1)
        ]

    for ch in range(chunks):
        for d in range(zn - 1, 2, -1):
            for sign, ok, _ in rows_at(d):
                go(ok, far, me, ch, sign, d)
        go(has_up, along, me, ch, 1)
        go(has_dn, along, me, ch, -1)
        go(None, across, me, ch)
        go(None, beside, me, ch)

    loads[3].wait()
    group = 4 * hdim
    queries = jnp.dot(normed, wqkv[:, 0:width], preferred_element_type=jnp.float32)
    queries = queries.astype(jnp.bfloat16) * jnp.bfloat16(hdim**-0.5)
    lane_head = (lax.broadcasted_iota(jnp.int32, queries.shape, 1) % group) // hdim
    for a in range(4):
        qmask[a * toks : (a + 1) * toks, :] = jnp.where(
            lane_head == a, queries, jnp.zeros_like(queries)
        )

    def line(d):
        for ch in range(chunks):
            for sign, ok, row in rows_at(d):
                block = row * 4 + me % 4
                pl.when(ok)(functools.partial(arrived, block, ch))
                if d == 1:
                    go(ok & (has_up if sign < 0 else has_dn), along, block, ch, -sign)
                go(ok, across, block, ch)
                go(ok, beside, block, ch)

    def pass_on(d):
        for ch in range(chunks):
            for _, ok, row in rows_at(d):
                block = row * 4 + other_x % 4
                if ok is None:
                    arrived(block, ch)
                else:
                    pl.when(ok)(functools.partial(arrived, block, ch))
                go(ok, beside, block, ch)

    def project(row):
        for ch in range(chunks):
            arrived(row * 4 + other_core % 4, ch)
            arrived(row * 4 + 2 * (1 - x_at) + 1 - core, ch)
        have = gat[pl.ds(row * 4, 4)].reshape(4 * toks, chans)
        kv = jnp.dot(have, wqkv[:, width:], preferred_element_type=jnp.float32)
        kv = kv.astype(jnp.bfloat16)
        keys[row] = kv[:, 0:width]
        vals[row] = kv[:, width:]

    def project_both(d):
        @pl.loop(0, 2)
        def _(t):
            row = z_at + d * (2 * t - 1)

            @pl.when((row >= 0) & (row < zn))
            def _():
                project(row)

    if zn > 1:
        line(1)
    pass_on(0)
    project(z_at)
    for d in range(1, zn):
        if d == 1:
            for later in range(2, zn):
                line(later)
        pass_on(d)
        if d > 1:
            project_both(d - 1)
    if zn > 1:
        project_both(zn - 1)

    for g in range(heads // 4):
        lanes = slice(g * group, (g + 1) * group)
        scores = lax.dot_general(
            qmask[:, lanes],
            keys[:, :, lanes].reshape(n * toks, group),
            (((1,), (1,)), ((), ())),
            preferred_element_type=jnp.float32,
        )
        raised = jnp.exp(scores - jnp.max(scores, axis=-1, keepdims=True))
        total = jnp.sum(raised, axis=-1, keepdims=True)
        weights = (raised * (1.0 / total)).astype(jnp.bfloat16)
        mixed = jnp.dot(
            weights,
            vals[:, :, lanes].reshape(n * toks, group),
            preferred_element_type=jnp.float32,
        )
        heads_at = lax.broadcasted_iota(jnp.int32, (toks, group), 1) // hdim
        got = mixed[0:toks]
        for a in range(1, 4):
            got = jnp.where(heads_at == a, mixed[a * toks : (a + 1) * toks], got)
        att[:, lanes] = got.astype(jnp.bfloat16)

    loads[4].wait()
    final = tokens + jnp.dot(att[...], wo[...], preferred_element_type=jnp.float32)
    out_ref[...] = final.reshape(out_ref.shape).astype(jnp.bfloat16)

    for cond, copy in sent:
        if cond is None:
            copy().wait_send()
        else:
            pl.when(cond)(lambda copy=copy: copy().wait_send())


def fast_body(n, surface_field, conv_a, conv_b, norm_gain, qkv_weight, out_weight):
    rows, cols, chans_in = surface_field.shape
    chans = conv_a.shape[-1]
    srows, tcols = rows // 4, cols // 4
    toks = srows * tcols
    width = out_weight.shape[0]
    heads, zn = width // HEAD_DIM, n // 4
    bf16, f32 = jnp.bfloat16, jnp.float32
    vm, anyw = pl.BlockSpec(memory_space=pltpu.VMEM), pl.BlockSpec(memory_space=pl.ANY)
    out = pl.pallas_call(
        functools.partial(fused_kernel, n, cols, toks, heads, HEAD_DIM),
        out_shape=jax.ShapeDtypeStruct((tcols, srows, chans), bf16),
        in_specs=[anyw, anyw, anyw, vm, anyw, anyw],
        out_specs=vm,
        scratch_shapes=[
            pltpu.VMEM((rows * cols, chans_in), bf16),
            pltpu.VMEM((9 * chans_in, chans), bf16),
            pltpu.VMEM((9 * chans, chans), bf16),
            pltpu.VMEM(qkv_weight.shape, bf16),
            pltpu.VMEM(out_weight.shape, bf16),
            pltpu.VMEM((chans_in // 128, (rows + 2) * cols, 128), f32),
            pltpu.VMEM((6, cols + 2, srows, chans_in), bf16),
            pltpu.VMEM((2, 4, srows, chans_in), bf16),
            pltpu.VMEM((2, 4, srows, chans_in), bf16),
            pltpu.VMEM((4, cols // 2 + 2, srows, chans), bf16),
            pltpu.VMEM((2, 2, srows, chans), bf16),
            pltpu.VMEM((2, 2, srows, chans), bf16),
            pltpu.VMEM((n, CHUNKS, toks // CHUNKS, chans), bf16),
            pltpu.VMEM((zn, 4 * toks, width), bf16),
            pltpu.VMEM((zn, 4 * toks, width), bf16),
            pltpu.VMEM((4 * toks, width), bf16),
            pltpu.VMEM((toks, width), bf16),
            pltpu.SemaphoreType.DMA((5,)),
            pltpu.SemaphoreType.DMA((4,)),
            pltpu.SemaphoreType.DMA((4,)),
            pltpu.SemaphoreType.DMA((2, zn, CHUNKS)),
            pltpu.SemaphoreType.DMA((2, zn, CHUNKS)),
            pltpu.SemaphoreType.DMA((zn, CHUNKS)),
            pltpu.SemaphoreType.DMA((2 * zn, CHUNKS)),
            pltpu.SemaphoreType.DMA((n, CHUNKS)),
        ],
        compiler_params=pltpu.CompilerParams(
            collective_id=0, has_side_effects=True, vmem_limit_bytes=60 * 2**20
        ),
    )(
        surface_field.reshape(rows * cols, chans_in),
        conv_a.reshape(9 * chans_in, chans),
        conv_b.reshape(9 * chans, chans),
        norm_gain.reshape(1, chans),
        qkv_weight,
        out_weight,
    )
    return out.transpose(1, 0, 2)


def solution(mesh):
    n = mesh.shape["lon"]
    plain = mesh.shape["lat"] > 1 or n % 4 or n < 4 or n > 16
    run = body if plain else functools.partial(fast_body, n)
    in_specs = (P(("grp", "lat"), "lon", None), P(), P(), P(), P(), P())
    out_specs = P(("grp", "lat"), "lon", None)
    return jax.shard_map(run, mesh=mesh, in_specs=in_specs, out_specs=out_specs, check_vma=False)
```

profile of v0, /device:TPU:0, one launch (start us, length us, event | category | flops | bytes accessed | tf_op | source)
XLA Modules:
  0.0 33.7 jit_solution(432874914146565888)
XLA Ops:
  0.0 32.2 %shard_map.64 = bf16[2,32,512]{2,1,0:T(8,128)(2,1)} custom-call(bf16[1024,256]{1,0:T(8,128)(2,1)} %bitcast.7, bf16[2304,512]{1,0:T(8,128)(2,1)} %bitcast.6, bf16[4608,512]{1,0:T(8,128)(2,1)} %bitcast.5, f32[1,512]{1,0:T(1,128)} %bitcast.9, bf16[512,3072]{1,0:T(8,128)(2,1)} %wqkv_hbm.1, bf16[1024,512]{1,0:T(8,128)(2,1)} %wo_hbm.1), custom_call_target="tpu_custom_call" | custom-call | tf_op jit(solution)/shard_map/pallas_call | solution.py:480
  32.2 1.5 %copy.7 = bf16[32,2,512]{2,1,0:T(2,128)(2,1)} copy(bf16[32,2,512]{2,0,1:T(8,128)(2,1)} %bitcast.8) | data formatting | bytes 131072 | tf_op jit(solution)/shard_map/transpose | solution.py:523
where the time goes:
time: 33.9 us; the launch traced here: 33.7 us
  Pallas kernels  32.2 us (95%)
  local copies, waits for them, and re-layouts  1.54 us (5%)
    pallas_call x1, Pallas kernels, fast_body(): pl.pallas_call(functools.partial(fused_kernel, n, cols, toks, heads, HEAD...  32.2 us
    transpose x1, local copies, waits for them, and re-layouts, fast_body(): return out.transpose(1, 0, 2)  1.54 us

commit v1 on v0

--- a/solution.py
+++ b/solution.py
@@ -136,8 +136,8 @@
 
 def fused_kernel(
     n, cols, toks, heads, hdim,
-    x_hbm, wa_hbm, wb_hbm, gain_ref, wqkv_hbm, wo_hbm, out_ref,
-    x_v, wa, wb, wqkv, wo, xf, xs, edge_out, edge_in, ps, pedge_out, pedge_in,
+    x_hbm, wa_hbm, wb_hbm, gain_hbm, wqkv_hbm, wo_hbm, out_ref,
+    x_v, wa, wb, wqkv, wo, gain_ref, xf, xs, edge_out, edge_in, ps, pedge_out, pedge_in,
     gat, keys, vals, qmask, att,
     load_sem, halo_send, halo_recv, z_send, far_send, x_send, c_send, recv,
 ):
@@ -153,7 +153,7 @@
     loads = [
         pltpu.make_async_copy(s, d, load_sem.at[i])
         for i, (s, d) in enumerate(
-            ((x_hbm, x_v), (wa_hbm, wa), (wb_hbm, wb), (wqkv_hbm, wqkv), (wo_hbm, wo))
+            ((x_hbm, x_v), (wa_hbm, wa), (wb_hbm, wb), (wqkv_hbm, wqkv), (wo_hbm, wo), (gain_hbm, gain_ref))
         )
     ]
     for c in loads:
@@ -274,6 +274,7 @@
         return z.reshape(2, 2, srows, z.shape[-1])
 
     loads[2].wait()
+    loads[5].wait()
     chans = ps.shape[-1]
     inner = conv_second(
         jnp.concatenate(
@@ -476,11 +477,11 @@
     width = out_weight.shape[0]
     heads, zn = width // HEAD_DIM, n // 4
     bf16, f32 = jnp.bfloat16, jnp.float32
-    vm, anyw = pl.BlockSpec(memory_space=pltpu.VMEM), pl.BlockSpec(memory_space=pl.ANY)
+    vm, anyw = pl.BlockSpec(memory_space=pltpu.VMEM), pl.BlockSpec(memory_space=pltpu.HBM)
     out = pl.pallas_call(
         functools.partial(fused_kernel, n, cols, toks, heads, HEAD_DIM),
-        out_shape=jax.ShapeDtypeStruct((tcols, srows, chans), bf16),
-        in_specs=[anyw, anyw, anyw, vm, anyw, anyw],
+        out_shape=pltpu.VMEM((tcols, srows, chans), bf16),
+        in_specs=[anyw] * 6,
         out_specs=vm,
         scratch_shapes=[
             pltpu.VMEM((rows * cols, chans_in), bf16),
@@ -488,6 +489,7 @@
             pltpu.VMEM((9 * chans, chans), bf16),
             pltpu.VMEM(qkv_weight.shape, bf16),
             pltpu.VMEM(out_weight.shape, bf16),
+            pltpu.VMEM((1, chans), f32),
             pltpu.VMEM((chans_in // 128, (rows + 2) * cols, 128), f32),
             pltpu.VMEM((6, cols + 2, srows, chans_in), bf16),
             pltpu.VMEM((2, 4, srows, chans_in), bf16),
@@ -500,7 +502,7 @@
             pltpu.VMEM((zn, 4 * toks, width), bf16),
             pltpu.VMEM((4 * toks, width), bf16),
             pltpu.VMEM((toks, width), bf16),
-            pltpu.SemaphoreType.DMA((5,)),
+            pltpu.SemaphoreType.DMA((6,)),
             pltpu.SemaphoreType.DMA((4,)),
             pltpu.SemaphoreType.DMA((4,)),
             pltpu.SemaphoreType.DMA((2, zn, CHUNKS)),
@@ -510,15 +512,20 @@
             pltpu.SemaphoreType.DMA((n, CHUNKS)),
         ],
         compiler_params=pltpu.CompilerParams(
-            collective_id=0, has_side_effects=True, vmem_limit_bytes=60 * 2**20
+            collective_id=0, has_side_effects=True, vmem_limit_bytes=48 * 2**20
         ),
     )(
-        surface_field.reshape(rows * cols, chans_in),
-        conv_a.reshape(9 * chans_in, chans),
-        conv_b.reshape(9 * chans, chans),
-        norm_gain.reshape(1, chans),
-        qkv_weight,
-        out_weight,
+        *(
+            pltpu.with_memory_space_constraint(v, pltpu.HBM)
+            for v in (
+                surface_field.reshape(rows * cols, chans_in),
+                conv_a.reshape(9 * chans_in, chans),
+                conv_b.reshape(9 * chans, chans),
+                norm_gain.reshape(1, chans),
+                qkv_weight,
+                out_weight,
+            )
+        )
     )
     return out.transpose(1, 0, 2)
 

time: 33.9 us -> 31.7 us (0.935)
  Pallas kernels: 32.2 us -> 30.9 us
  local copies, waits for them, and re-layouts: 1.54 us -> 0.7 us
    pallas_call x1, Pallas kernels: 32.2 us -> 30.9 us  [fast_body(): pl.pallas_call(functools.partial(fused_kernel, n, cols, toks, heads, HEAD...]
    transpose x1, local copies, waits for them, and re-layouts: 1.54 us -> 0.7 us  [fast_body(): return out.transpose(1, 0, 2)]
where the time goes in v1:
time: 31.7 us; the launch traced here: 31.6 us
  Pallas kernels  30.9 us (97%)
  local copies, waits for them, and re-layouts  0.7 us (2%)
    pallas_call x1, Pallas kernels, fast_body(): pl.pallas_call(functools.partial(fused_kernel, n, cols, toks, heads, HEAD...  30.9 us
    transpose x1, local copies, waits for them, and re-layouts, fast_body(): return out.transpose(1, 0, 2)  0.7 us

profile of v1, /device:TPU:0, one launch (start us, length us, event | category | flops | bytes accessed | tf_op | source)
XLA Modules:
  0.0 31.6 jit_solution(10712666663191187038)
XLA Ops:
  0.0 30.9 %shard_map.64 = bf16[2,32,512]{2,1,0:T(8,128)(2,1)S(1)} custom-call(bf16[1024,256]{1,0:T(8,128)(2,1)} %bitcast.8, bf16[2304,512]{1,0:T(8,128)(2,1)} %bitcast.7, bf16[4608,512]{1,0:T(8,128)(2,1)} %bitcast.6, f32[1,512]{1,0:T(1,128)} %bitcast.9, bf16[512,3072]{1,0:T(8,128)(2,1)} %wqkv_hbm.1, bf16[1024,512]{1,0:T(8,128)(2,1)} %wo_hbm.1), custom_call_target="tpu_custom_call" | custom-call | tf_op jit(solution)/shard_map/pallas_call | solution.py:481
  30.9 0.7 %copy.7 = bf16[32,2,512]{2,1,0:T(2,128)(2,1)} copy(bf16[32,2,512]{2,0,1:T(8,128)(2,1)S(1)} %bitcast.5) | data formatting | bytes 131072 | tf_op jit(solution)/shard_map/transpose | solution.py:530

commit v2 on v1

v2 whole, which is shorter than its diff:
```python
import functools

import jax
import jax.numpy as jnp
from jax import lax
from jax.experimental import pallas as pl
from jax.experimental.pallas import tpu as pltpu
from jax.sharding import PartitionSpec as P

CB = 512
HEADS = 16
HEAD_DIM = 64
CHUNKS = 2


def with_halo(block, sides, width):
    for axis, dim in sides:
        count = lax.axis_size(axis)
        forward = [(i, i + 1) for i in range(count - 1)]
        forward.append((count - 1, 0))
        backward = [(target, source) for source, target in forward]
        low = lax.ppermute(
            lax.slice_in_dim(block, block.shape[dim] - width, None, axis=dim), axis, forward
        )
        high = lax.ppermute(lax.slice_in_dim(block, 0, width, axis=dim), axis, backward)
        block = jnp.concatenate([low, block, high], axis=dim)
    return block


def partner_2(value, axis, distance):
    mask = 2**distance
    pairs = [(source, source ^ mask) for source in range(lax.axis_size(axis))]
    return lax.ppermute(value, axis, pairs)


def convolve(values_in, weight):
    return lax.conv_general_dilated(
        values_in[None],
        weight,
        (1, 1),
        "VALID",
        dimension_numbers=("NHWC", "HWIO", "NHWC"),
        preferred_element_type=jnp.float32,
    )[0]


def average_pool(values_in):
    rows_in, cols_in, chans_in = values_in.shape
    return values_in.reshape(rows_in // 2, 2, cols_in // 2, 2, chans_in).mean(axis=(1, 3))


def layer_norm(tokens_flat, norm_gain):
    centred = tokens_flat - jnp.mean(tokens_flat, axis=-1, keepdims=True)
    spread = jnp.mean(centred * centred, axis=-1, keepdims=True)
    return centred * lax.rsqrt(spread + 0.01) * norm_gain


def softmax_rows(scores):
    maxima = jnp.max(scores, axis=-1, keepdims=True)
    raised = jnp.exp(scores - maxima)
    return raised / jnp.sum(raised, axis=-1, keepdims=True)


def keep_rows(values_in, rows_here, lat_count, lat_where, margin):
    first_row = lat_where * rows_here - margin
    rowpos = first_row + jnp.arange(values_in.shape[0], dtype=jnp.int32)
    inside = (rowpos >= 0) & (rowpos < rows_here * lat_count)
    return jnp.where(inside[:, None, None], values_in, jnp.zeros((), values_in.dtype))


def body(surface_field, conv_a, conv_b, norm_gain, qkv_weight, out_weight):
    lon_count = lax.axis_size("lon")
    lat_count = lax.axis_size("lat")
    lat_where = lax.axis_index("lat")
    rows_here = surface_field.shape[0]
    padded_field = with_halo(surface_field, (("lon", 1), ("lat", 0)), 1)
    padded_field = keep_rows(padded_field, rows_here, lat_count, lat_where, 1)
    first_out = jax.nn.silu(convolve(padded_field, conv_a))
    pooled_first = average_pool(first_out).astype(jnp.bfloat16)
    ready_rows = with_halo(pooled_first, (("lon", 1), ("lat", 0)), 1)
    ready_rows = keep_rows(ready_rows, rows_here // 2, lat_count, lat_where, 1)
    second_out = jax.nn.silu(convolve(ready_rows, conv_b))
    pooled_second = average_pool(second_out)
    tok_rows, tok_cols = (pooled_second.shape[0], pooled_second.shape[1])
    local_tokens = tok_rows * tok_cols
    tokens_flat = pooled_second.reshape(local_tokens, CB)
    normed = layer_norm(tokens_flat, norm_gain).astype(jnp.bfloat16)
    projected = jnp.dot(normed, qkv_weight, preferred_element_type=jnp.float32).astype(jnp.bfloat16)
    residues = max(1, lon_count // HEADS)
    groups = lon_count // residues
    per_slot = HEADS // groups
    per_residue = local_tokens // residues
    arranged = projected.reshape(per_residue, residues, 3, groups, per_slot, HEAD_DIM)
    outgoing = arranged.transpose(2, 1, 3, 4, 0, 5).reshape(
        3, lon_count, per_slot, per_residue, HEAD_DIM
    )
    swap_bits = list(range(groups.bit_length() - 1, lon_count.bit_length() - 1))
    arrived = lax.all_to_all(outgoing, "lon", split_axis=1, concat_axis=3, tiled=True)
    queries = arrived[0, 0]
    keys_vals = arrived[1:, 0]
    for bit_pos in swap_bits:
        partner = partner_2(keys_vals, "lon", bit_pos)
        keys_vals = jnp.concatenate([keys_vals, partner], axis=2)
    for bit_pos in range(lat_count.bit_length() - 1):
        partner = partner_2(keys_vals, "lat", bit_pos)
        keys_vals = jnp.concatenate([keys_vals, partner], axis=2)
    score_scale = HEAD_DIM ** (-0.5)
    scores = (
        jnp.einsum("hqd,hkd->hqk", queries, keys_vals[0], preferred_element_type=jnp.float32)
        * score_scale
    )
    weights = softmax_rows(scores).astype(jnp.bfloat16)
    head_out = jnp.einsum(
        "hqk,hkd->hqd", weights, keys_vals[1], preferred_element_type=jnp.float32
    ).astype(jnp.bfloat16)
    returned = lax.all_to_all(head_out[None], "lon", split_axis=2, concat_axis=0, tiled=True)
    attended = returned.reshape(residues, groups, per_slot, per_residue, HEAD_DIM).transpose(
        3, 0, 1, 2, 4
    )
    attended = attended.reshape(local_tokens, HEADS * HEAD_DIM)
    mixed_out = tokens_flat + jnp.dot(attended, out_weight, preferred_element_type=jnp.float32)
    return mixed_out.reshape(tok_rows, tok_cols, CB).astype(jnp.bfloat16)


def roll_rows(values, amount):
    count = values.shape[0]
    moved = pltpu.roll(values, amount % count, 0)
    rowpos = lax.broadcasted_iota(jnp.int32, values.shape, 0)
    edge = 0 if amount == 1 else count - 1
    return jnp.where(rowpos == edge, jnp.zeros_like(moved), moved)


def silu(v):
    half = 0.5 * v
    return half + half * jnp.tanh(half)


def fused_kernel(
    n, cols, toks, heads, hdim,
    x_hbm, wa_hbm, wb_hbm, gain_hbm, wqkv_hbm, wo_hbm, out_ref,
    x_v, wa, wb, wqkv, wo, gain_ref, xs, edge_in, ps, pedge_out, pedge_in,
    gat, sums, totals, peaks, qmask, att,
    load_sem, near_ok, halo_send, halo_recv, block_send, block_recv, side_recv,
):
    width = heads * hdim
    me = lax.axis_index("lon")
    core, x_at, z_at = me % 2, (me // 2) % 2, me // 4
    other_core = me + 1 - 2 * core
    other_x = me + 2 - 4 * x_at
    beyond = (me + n - 1 + 2 * core) % n
    wraps = me // (n - 1) + (n - 1 - me) // (n - 1)
    first, last = me == 0, me == n - 1
    wrap, inner = first | last, (me > 0) & (me < n - 1)
    near, two = z_at + 1 - 2 * (z_at // 2), (z_at + 2) % 4
    rest = (near + 2) % 4
    ends = z_at // 3 + (3 - z_at) // 3
    middle, edge = (z_at > 0) & (z_at < 3), (z_at == 0) | (z_at == 3)
    own, mate = me % 4, other_x % 4

    loads = [
        pltpu.make_async_copy(s, d, load_sem.at[i])
        for i, (s, d) in enumerate(
            (
                (x_hbm, x_v), (wa_hbm, wa), (wb_hbm, wb),
                (gain_hbm, gain_ref), (wqkv_hbm, wqkv), (wo_hbm, wo),
            )
        )
    ]
    for c in loads:
        c.start()

    barrier = pltpu.get_barrier_semaphore()

    def greet(dev):
        pl.semaphore_signal(barrier, inc=1, device_id={"lon": dev})

    for dev in (beyond, other_core, other_x, two * 4 + own, near * 4 + own, near * 4 + mate):
        greet(dev)

    @pl.when(middle)
    def _():
        greet(rest * 4 + own)
        greet(rest * 4 + mate)

    greeted = 8 - 2 * ends

    srows = x_v.shape[0] // cols // 4
    span = 32 * cols
    row = lax.broadcasted_iota(jnp.int32, (span, span), 0)
    col = lax.broadcasted_iota(jnp.int32, (span, span), 1)
    source = (4 * (row % 8) + row // (8 * cols)) * cols + (row // 8) % cols
    order = jnp.where(col == source, 1.0, 0.0).astype(jnp.bfloat16)
    loads[0].wait()
    turned = [
        jnp.dot(order, x_v[at : at + span, :], preferred_element_type=jnp.float32)
        for at in range(0, x_v.shape[0], span)
    ]

    def column(k, j):
        at = (k * cols + j) * 8
        return jnp.concatenate([t[at : at + 8] for t in turned], axis=0)

    for j in range(cols):
        for k in range(4):
            xs[k + 1, j + 3] = column(k, j).astype(jnp.bfloat16)

    def halo(i, k, src, dst, dev):
        return pltpu.make_async_remote_copy(
            src_ref=src,
            dst_ref=dst,
            send_sem=halo_send.at[k],
            recv_sem=halo_recv.at[i],
            device_id={"lon": dev},
        )

    def edge_column(j):
        return xs.at[pl.ds(1, 4), j + 3]

    by_near = halo(3, 0, edge_column((1 - core) * (cols - 1)), edge_in.at[3], other_core)
    by_far = [
        halo(
            min(i, 1), 0, edge_column(core * (cols - 1) + (1 - 2 * core) * i), edge_in.at[i], beyond
        )
        for i in range(3)
    ]
    by_near_2 = halo(4, 1, pedge_out.at[0], pedge_in.at[0], other_core)
    by_far_2 = halo(2, 1, pedge_out.at[1], pedge_in.at[1], beyond)

    @pl.when(me > 0)
    def _():
        pl.semaphore_wait(barrier, greeted)

    @pl.when(first)
    def _():
        pl.semaphore_wait(near_ok, 1)

    @pl.when(me == 1)
    def _():
        pl.semaphore_signal(near_ok, inc=1, device_id={"lon": other_core})

    @pl.when(me > 0)
    def _():
        by_far[0].start()

    by_near.start()

    @pl.when(last)
    def _():
        by_far[1].start()
        by_far[2].start()

    for j in range(cols):
        xs[0, j + 3] = roll_rows(column(3, j), 1).astype(jnp.bfloat16)
        xs[5, j + 3] = roll_rows(column(0, j), -1).astype(jnp.bfloat16)

    pcols = cols // 2

    def conv_first(*jps):
        taps = [
            jnp.concatenate(
                [
                    xs[a : a + 4, pl.ds(2 * jp + 2 + b, 2)].reshape(8 * srows, xs.shape[-1])
                    for jp in jps
                ],
                axis=0,
            )
            for a in range(3)
            for b in range(3)
        ]
        y = silu(
            jnp.dot(jnp.concatenate(taps, axis=1), wa[...], preferred_element_type=jnp.float32)
        )
        y = y.reshape(len(jps), 4, 2, srows, y.shape[-1])
        return [
            [
                (y[i, k, 0] + y[i, k, 1] + y[i, k + 1, 0] + y[i, k + 1, 1]) * 0.25
                for k in (0, 2)
            ]
            for i in range(len(jps))
        ]

    def put_pooled(at, even, odd):
        ps[0, at] = roll_rows(odd, 1).astype(jnp.bfloat16)
        ps[1, at] = even.astype(jnp.bfloat16)
        ps[2, at] = odd.astype(jnp.bfloat16)
        ps[3, at] = roll_rows(even, -1).astype(jnp.bfloat16)

    def put_edge(side, even, odd):
        pedge_out[side, 0] = even.astype(jnp.bfloat16)
        pedge_out[side, 1] = odd.astype(jnp.bfloat16)

    def put_column(i, at):
        for k in range(4):
            xs[k + 1, at] = edge_in[i, k]
        xs[0, at] = roll_rows(edge_in[i, 3].astype(jnp.float32), 1).astype(jnp.bfloat16)
        xs[5, at] = roll_rows(edge_in[i, 0].astype(jnp.float32), -1).astype(jnp.bfloat16)

    def put_far(i):
        put_column(i, 2 - i + core * (cols + 1 + 2 * i))

    jp_near, jp_far = (1 - core) * (pcols - 1), core * (pcols - 1)
    jp_third = jp_far + wraps * (2 - jp_far)
    jp_fourth = 2 + jp_far - jp_third
    loads[1].wait()
    by_near.wait_recv()
    put_column(3, (1 - core) * (cols + 1) + 2)
    inside, beside_near = conv_first(1, jp_near)
    put_pooled(jp_near + 1, *beside_near)
    put_edge(0, *beside_near)
    put_pooled(2, *inside)
    by_near_2.start()

    @pl.when(first)
    def _():
        pl.semaphore_wait(barrier, greeted)
        for copy in by_far:
            copy.start()

    @pl.when(inner)
    def _():
        by_far[0].wait_recv()
        put_far(0)

    (third,) = conv_first(jp_third)
    put_edge(1, *third)
    put_pooled(jp_third + 1, *third)

    @pl.when(inner)
    def _():
        by_far_2.start()

    @pl.when(wrap)
    def _():
        by_far[0].wait_recv()
        put_far(0)

    def conv_second(pieces):
        z = silu(jnp.dot(pieces, wb[...], preferred_element_type=jnp.float32))
        return z.reshape(2, 2, srows, z.shape[-1])

    loads[2].wait()
    loads[3].wait()
    (fourth,) = conv_first(jp_fourth)
    put_pooled(jp_fourth + 1, *fourth)
    chans = ps.shape[-1]
    inside = conv_second(
        jnp.concatenate(
            [
                ps[a : a + 2, 1 + b : 3 + b].reshape(4 * srows, chans)
                for a in range(3)
                for b in range(3)
            ],
            axis=1,
        )
    )
    by_near_2.wait_recv()
    put_pooled(
        (1 - core) * (pcols + 1),
        pedge_in[0, 0].astype(jnp.float32),
        pedge_in[0, 1].astype(jnp.float32),
    )
    far_at = core * (pcols + 1)

    @pl.when(inner)
    def _():
        by_far_2.wait_recv()
        put_pooled(
            far_at, pedge_in[1, 0].astype(jnp.float32), pedge_in[1, 1].astype(jnp.float32)
        )

    @pl.when(wrap)
    def _():
        both = edge_in.at[pl.ds(1, 2)]
        halo(1, 0, both, both, beyond).wait_recv()
        put_far(1)
        put_far(2)
        put_pooled(far_at, *conv_first(core * (pcols + 1) - 1)[0])

    outer = conv_second(
        jnp.concatenate(
            [
                jnp.concatenate(
                    [
                        ps[a : a + 2, b].reshape(2 * srows, chans),
                        ps[a : a + 2, pcols - 1 + b].reshape(2 * srows, chans),
                    ],
                    axis=0,
                )
                for a in range(3)
                for b in range(3)
            ],
            axis=1,
        )
    )
    tokens = jnp.concatenate(
        [
            (inside[0, side] + inside[1, side] + outer[side, 0] + outer[side, 1]) * 0.25
            for side in range(2)
        ],
        axis=0,
    )
    centred = tokens - jnp.mean(tokens, axis=-1, keepdims=True)
    spread = jnp.mean(centred * centred, axis=-1, keepdims=True)
    normed = (centred * lax.rsqrt(spread + 0.01) * gain_ref[...]).astype(jnp.bfloat16)
    chunks = gat.shape[1]
    gat[me] = normed.reshape(gat.shape[1:])

    def send(block, ch, dev, sem):
        return pltpu.make_async_remote_copy(
            src_ref=gat.at[block, ch],
            dst_ref=gat.at[block, ch],
            send_sem=block_send,
            recv_sem=sem,
            device_id={"lon": dev},
        )

    def go(block, ch, dev):
        send(block, ch, dev, block_recv.at[block // 2, ch]).start()

    def beside(block, ch, unit):
        send(block, ch, other_core, side_recv.at[unit]).start()

    def arrived(block, ch):
        send(block, ch, other_core, block_recv.at[block // 2, ch]).wait_recv()

    for ch in range(chunks):
        go(me, ch, two * 4 + own)
        go(me, ch, other_x)
        beside(me, ch, 0)

    @pl.when(middle)
    def _():
        for ch in range(chunks):
            go(me, ch, rest * 4 + own)

    for ch in range(chunks):
        go(me, ch, near * 4 + mate)
    for ch in range(chunks):
        go(me, ch, near * 4 + own)

    loads[4].wait()
    group = 4 * hdim
    queries = jnp.dot(normed, wqkv[:, 0:width], preferred_element_type=jnp.float32)
    queries = queries.astype(jnp.bfloat16) * jnp.bfloat16(hdim**-0.5)
    lane_head = (lax.broadcasted_iota(jnp.int32, queries.shape, 1) % group) // hdim
    for a in range(4):
        qmask[a * toks : (a + 1) * toks, :] = jnp.where(
            lane_head == a, queries, jnp.zeros_like(queries)
        )
    heads_at = lax.broadcasted_iota(jnp.int32, (toks, group), 1) // hdim

    def by_head(v):
        got = v[0:toks]
        for a in range(1, 4):
            got = jnp.where(heads_at == a, v[a * toks : (a + 1) * toks], got)
        return got

    def attend(unit, chips, start=False, end=False):
        count = len(chips)
        both = gat.at[pl.ds(0, count)]
        pltpu.make_async_remote_copy(
            src_ref=both,
            dst_ref=both,
            send_sem=block_send,
            recv_sem=side_recv.at[unit],
            device_id={"lon": other_core},
        ).wait_recv()
        have = jnp.concatenate(
            [gat[pl.ds(2 * c, 2)].reshape(2 * toks, chans) for c in chips], axis=0
        )
        keys, vals, mixes, norms = {}, {}, {}, {}

        def project(g):
            for held, at in ((keys, width), (vals, 2 * width)):
                at = at + g * group
                made = jnp.dot(have, wqkv[:, at : at + group], preferred_element_type=jnp.float32)
                held[g] = made.astype(jnp.bfloat16)

        def score(g):
            scores = lax.dot_general(
                qmask[:, g * group : (g + 1) * group],
                keys[g],
                (((1,), (1,)), ((), ())),
                preferred_element_type=jnp.float32,
            )
            peak = jnp.max(scores, axis=-1, keepdims=True)
            raised = jnp.exp(scores - peak)
            norms[g] = peak, jnp.sum(raised, axis=-1, keepdims=True)
            mixes[g] = raised.astype(jnp.bfloat16)

        def mix(g):
            lanes = slice(g * group, (g + 1) * group)
            mixed = jnp.dot(mixes[g], vals[g], preferred_element_type=jnp.float32)
            got, peak, total = by_head(mixed), by_head(norms[g][0]), by_head(norms[g][1])
            if not start:
                top = jnp.maximum(peaks[:, lanes], peak)
                was, now = jnp.exp(peaks[:, lanes] - top), jnp.exp(peak - top)
                got = sums[:, lanes] * was + got * now
                total = totals[:, lanes] * was + total * now
                peak = top
            if end:
                att[:, lanes] = (got * (1.0 / total)).astype(jnp.bfloat16)
            else:
                sums[:, lanes], totals[:, lanes], peaks[:, lanes] = got, total, peak

        groups = heads // 4
        for step in range(groups + 2):
            if step < groups:
                project(step)
            if 0 <= step - 1 < groups:
                score(step - 1)
            if 0 <= step - 2 < groups:
                mix(step - 2)

    b_near, b_two, b_rest = near * 4 + own, two * 4 + own, rest * 4 + own
    c_near, c_two, c_rest = near * 4 + mate, two * 4 + mate, rest * 4 + mate

    def take(block, ch, unit, *onward):
        arrived(block, ch)
        for dev in onward:
            go(block, ch, dev)
        beside(block, ch, unit)

    def take_two(ch):
        arrived(b_two, ch)

        @pl.when(middle)
        def _():
            go(b_two, ch, rest * 4 + own)
            go(b_two, ch, rest * 4 + mate)

        go(b_two, ch, other_x)
        beside(b_two, ch, 3 - ends)

    def either(at_middle, at_end):
        return (at_middle + ends * (at_end - at_middle)) // 2

    attend(0, [me // 2], start=True)
    take(other_x, 0, 1)

    @pl.when(edge)
    def _():
        take(b_near, 0, 1, other_x)

    take(other_x, 1, 1)

    @pl.when(edge)
    def _():
        take(b_near, 1, 1, other_x)

    take_two(0)
    take_two(1)

    @pl.when(middle)
    def _():
        for ch in range(chunks):
            take(c_near, ch, 1)
            take(c_rest, ch, 2)
        for ch in range(chunks):
            take(b_rest, ch, 3)
            take(b_near, ch, 2)

    attend(1, [other_x // 2, either(c_near, b_near)])

    @pl.when(edge)
    def _():
        take(c_near, 0, 2)
        take(c_near, 1, 2)
        take(b_rest, 0, 3)

    take(c_two, 0, 4 - ends)
    take(c_two, 1, 4 - ends)

    @pl.when(edge)
    def _():
        take(b_rest, 1, 3)

    attend(2, [either(c_rest, b_two), either(b_near, c_near)])

    @pl.when(edge)
    def _():
        take(c_rest, 0, 4)
        take(c_rest, 1, 4)

    attend(3, [b_rest // 2, either(b_two, c_two)])
    attend(4, [either(c_two, c_rest)], end=True)

    loads[5].wait()
    final = tokens + jnp.dot(att[...], wo[...], preferred_element_type=jnp.float32)
    out_ref[...] = final.reshape(out_ref.shape).astype(jnp.bfloat16)

    def drain(ref, sem):
        pltpu.make_async_remote_copy(
            src_ref=ref,
            dst_ref=ref,
            send_sem=sem,
            recv_sem=halo_recv.at[0],
            device_id={"lon": other_core},
        ).wait_send()

    @pl.when(inner)
    def _():
        drain(edge_in.at[pl.ds(0, 2)], halo_send.at[0])
        drain(pedge_in, halo_send.at[1])

    @pl.when(wrap)
    def _():
        drain(edge_in, halo_send.at[0])
        drain(pedge_in.at[0], halo_send.at[1])

    @pl.when(middle)
    def _():
        drain(gat, block_send)

    @pl.when(edge)
    def _():
        drain(gat.at[pl.ds(0, n - 2)], block_send)


def fast_body(n, surface_field, conv_a, conv_b, norm_gain, qkv_weight, out_weight):
    rows, cols, chans_in = surface_field.shape
    chans = conv_a.shape[-1]
    srows, tcols = rows // 4, cols // 4
    toks = srows * tcols
    width = out_weight.shape[0]
    heads = width // HEAD_DIM
    bf16, f32 = jnp.bfloat16, jnp.float32
    vm, anyw = pl.BlockSpec(memory_space=pltpu.VMEM), pl.BlockSpec(memory_space=pltpu.HBM)
    out = pl.pallas_call(
        functools.partial(fused_kernel, n, cols, toks, heads, HEAD_DIM),
        out_shape=pltpu.VMEM((tcols, srows, chans), bf16),
        in_specs=[anyw] * 6,
        out_specs=vm,
        scratch_shapes=[
            pltpu.VMEM((rows * cols, chans_in), bf16),
            pltpu.VMEM((9 * chans_in, chans), bf16),
            pltpu.VMEM((9 * chans, chans), bf16),
            pltpu.VMEM(qkv_weight.shape, bf16),
            pltpu.VMEM(out_weight.shape, bf16),
            pltpu.VMEM((1, chans), f32),
            pltpu.VMEM((6, cols + 6, srows, chans_in), bf16),
            pltpu.VMEM((4, 4, srows, chans_in), bf16),
            pltpu.VMEM((4, cols // 2 + 2, srows, chans), bf16),
            pltpu.VMEM((2, 2, srows, chans), bf16),
            pltpu.VMEM((2, 2, srows, chans), bf16),
            pltpu.VMEM((n, CHUNKS, toks // CHUNKS, chans), bf16),
            pltpu.VMEM((toks, width), f32),
            pltpu.VMEM((toks, width), f32),
            pltpu.VMEM((toks, width), f32),
            pltpu.VMEM((4 * toks, width), bf16),
            pltpu.VMEM((toks, width), bf16),
            pltpu.SemaphoreType.DMA((6,)),
            pltpu.SemaphoreType.REGULAR,
            pltpu.SemaphoreType.DMA((2,)),
            pltpu.SemaphoreType.DMA((5,)),
            pltpu.SemaphoreType.DMA,
            pltpu.SemaphoreType.DMA((n // 2, CHUNKS)),
            pltpu.SemaphoreType.DMA((5,)),
        ],
        compiler_params=pltpu.CompilerParams(
            collective_id=0, has_side_effects=True, vmem_limit_bytes=48 * 2**20
        ),
    )(
        *(
            pltpu.with_memory_space_constraint(v, pltpu.HBM)
            for v in (
                surface_field.reshape(rows * cols, chans_in),
                conv_a.reshape(9 * chans_in, chans),
                conv_b.reshape(9 * chans, chans),
                norm_gain.reshape(1, chans),
                qkv_weight,
                out_weight,
            )
        )
    )
    return out.transpose(1, 0, 2)


def solution(mesh):
    n = mesh.shape["lon"]
    plain = mesh.shape["lat"] > 1 or n != 16
    run = body if plain else functools.partial(fast_body, n)
    in_specs = (P(("grp", "lat"), "lon", None), P(), P(), P(), P(), P())
    out_specs = P(("grp", "lat"), "lon", None)
    return jax.shard_map(run, mesh=mesh, in_specs=in_specs, out_specs=out_specs, check_vma=False)
```

time: 31.7 us -> 28 us (0.88)
  Pallas kernels: 30.9 us -> 27.2 us
    pallas_call x1, Pallas kernels: 30.9 us -> 27.2 us  [fast_body(): pl.pallas_call(functools.partial(fused_kernel, n, cols, toks, heads, HEAD...]
where the time goes in v2:
time: 28 us; the launch traced here: 27.9 us
  Pallas kernels  27.2 us (97%)
  local copies, waits for them, and re-layouts  0.7 us (2%)
    pallas_call x1, Pallas kernels, fast_body(): pl.pallas_call(functools.partial(fused_kernel, n, cols, toks, heads, HEAD...  27.2 us
    transpose x1, local copies, waits for them, and re-layouts, fast_body(): return out.transpose(1, 0, 2)  0.7 us

profile of v2, /device:TPU:0, one launch (start us, length us, event | category | flops | bytes accessed | tf_op | source)
XLA Modules:
  0.0 27.9 jit_solution(4761911125966047831)
XLA Ops:
  0.0 27.2 %shard_map.64 = bf16[2,32,512]{2,1,0:T(8,128)(2,1)S(1)} custom-call(bf16[1024,256]{1,0:T(8,128)(2,1)} %bitcast.8, bf16[2304,512]{1,0:T(8,128)(2,1)} %bitcast.7, bf16[4608,512]{1,0:T(8,128)(2,1)} %bitcast.6, f32[1,512]{1,0:T(1,128)} %bitcast.9, bf16[512,3072]{1,0:T(8,128)(2,1)} %wqkv_hbm.1, bf16[1024,512]{1,0:T(8,128)(2,1)} %wo_hbm.1), custom_call_target="tpu_custom_call" | custom-call | tf_op jit(solution)/shard_map/pallas_call | solution.py:629
  27.2 0.7 %copy.7 = bf16[32,2,512]{2,1,0:T(2,128)(2,1)} copy(bf16[32,2,512]{2,0,1:T(8,128)(2,1)S(1)} %bitcast.5) | data formatting | bytes 131072 | tf_op jit(solution)/shard_map/transpose | solution.py:676

commit v3 on v2

--- a/solution.py
+++ b/solution.py
@@ -139,8 +139,8 @@
     n, cols, toks, heads, hdim,
     x_hbm, wa_hbm, wb_hbm, gain_hbm, wqkv_hbm, wo_hbm, out_ref,
     x_v, wa, wb, wqkv, wo, gain_ref, xs, edge_in, ps, pedge_out, pedge_in,
-    gat, sums, totals, peaks, qmask, att,
-    load_sem, near_ok, halo_send, halo_recv, block_send, block_recv, side_recv,
+    gat, keys, vals, sums, totals, peaks, qmask, att,
+    load_sem, near_ok, told, halo_send, halo_recv, block_send, block_recv, side_recv,
 ):
     width = heads * hdim
     me = lax.axis_index("lon")
@@ -174,15 +174,8 @@
     def greet(dev):
         pl.semaphore_signal(barrier, inc=1, device_id={"lon": dev})
 
-    for dev in (beyond, other_core, other_x, two * 4 + own, near * 4 + own, near * 4 + mate):
-        greet(dev)
-
-    @pl.when(middle)
-    def _():
-        greet(rest * 4 + own)
-        greet(rest * 4 + mate)
-
-    greeted = 8 - 2 * ends
+    greet(other_core)
+    greet(beyond)
 
     srows = x_v.shape[0] // cols // 4
     span = 32 * cols
@@ -228,7 +221,7 @@
 
     @pl.when(me > 0)
     def _():
-        pl.semaphore_wait(barrier, greeted)
+        pl.semaphore_wait(barrier, 2)
 
     @pl.when(first)
     def _():
@@ -249,6 +242,23 @@
         by_far[1].start()
         by_far[2].start()
 
+    def tell(level):
+        step = 2**level
+        for way, dev, real in ((0, me + step, me < n - step), (1, me - step, me >= step)):
+
+            @pl.when(real)
+            def _(way=way, dev=dev):
+                pl.semaphore_signal(told.at[level, way], inc=1, device_id={"lon": dev})
+
+    def hear(level):
+        step = 2**level
+        for way, real in ((1, me < n - step), (0, me >= step)):
+
+            @pl.when(real)
+            def _(way=way):
+                pl.semaphore_wait(told.at[level, way], 1)
+
+    tell(0)
     for j in range(cols):
         xs[0, j + 3] = roll_rows(column(3, j), 1).astype(jnp.bfloat16)
         xs[5, j + 3] = roll_rows(column(0, j), -1).astype(jnp.bfloat16)
@@ -310,9 +320,12 @@
     put_pooled(2, *inside)
     by_near_2.start()
 
+    hear(0)
+    tell(1)
+
     @pl.when(first)
     def _():
-        pl.semaphore_wait(barrier, greeted)
+        pl.semaphore_wait(barrier, 2)
         for copy in by_far:
             copy.start()
 
@@ -328,6 +341,9 @@
     @pl.when(inner)
     def _():
         by_far_2.start()
+
+    hear(1)
+    tell(2)
 
     @pl.when(wrap)
     def _():
@@ -353,6 +369,7 @@
             axis=1,
         )
     )
+    hear(2)
     by_near_2.wait_recv()
     put_pooled(
         (1 - core) * (pcols + 1),
@@ -455,9 +472,8 @@
             got = jnp.where(heads_at == a, v[a * toks : (a + 1) * toks], got)
         return got
 
-    def attend(unit, chips, start=False, end=False):
-        count = len(chips)
-        both = gat.at[pl.ds(0, count)]
+    def project(unit, slot, chips):
+        both = gat.at[pl.ds(0, len(chips))]
         pltpu.make_async_remote_copy(
             src_ref=both,
             dst_ref=both,
@@ -468,18 +484,21 @@
         have = jnp.concatenate(
             [gat[pl.ds(2 * c, 2)].reshape(2 * toks, chans) for c in chips], axis=0
         )
-        keys, vals, mixes, norms = {}, {}, {}, {}
-
-        def project(g):
-            for held, at in ((keys, width), (vals, 2 * width)):
-                at = at + g * group
-                made = jnp.dot(have, wqkv[:, at : at + group], preferred_element_type=jnp.float32)
-                held[g] = made.astype(jnp.bfloat16)
+        made = jnp.dot(have, wqkv[:, width:], preferred_element_type=jnp.float32)
+        made = made.astype(jnp.bfloat16)
+        at = slice(slot * 2 * toks, (slot + len(chips)) * 2 * toks)
+        keys[at] = made[:, 0:width]
+        vals[at] = made[:, width:]
+
+    def attend(slots, end):
+        at = slice(slots[0] * 2 * toks, slots[1] * 2 * toks)
+        mixes, norms = {}, {}
 
         def score(g):
+            lanes = slice(g * group, (g + 1) * group)
             scores = lax.dot_general(
-                qmask[:, g * group : (g + 1) * group],
-                keys[g],
+                qmask[:, lanes],
+                keys[at, lanes],
                 (((1,), (1,)), ((), ())),
                 preferred_element_type=jnp.float32,
             )
@@ -490,27 +509,23 @@
 
         def mix(g):
             lanes = slice(g * group, (g + 1) * group)
-            mixed = jnp.dot(mixes[g], vals[g], preferred_element_type=jnp.float32)
+            mixed = jnp.dot(mixes[g], vals[at, lanes], preferred_element_type=jnp.float32)
             got, peak, total = by_head(mixed), by_head(norms[g][0]), by_head(norms[g][1])
-            if not start:
+            if end:
                 top = jnp.maximum(peaks[:, lanes], peak)
                 was, now = jnp.exp(peaks[:, lanes] - top), jnp.exp(peak - top)
                 got = sums[:, lanes] * was + got * now
                 total = totals[:, lanes] * was + total * now
-                peak = top
-            if end:
                 att[:, lanes] = (got * (1.0 / total)).astype(jnp.bfloat16)
             else:
                 sums[:, lanes], totals[:, lanes], peaks[:, lanes] = got, total, peak
 
         groups = heads // 4
-        for step in range(groups + 2):
+        for step in range(groups + 1):
             if step < groups:
-                project(step)
-            if 0 <= step - 1 < groups:
-                score(step - 1)
-            if 0 <= step - 2 < groups:
-                mix(step - 2)
+                score(step)
+            if step > 0:
+                mix(step - 1)
 
     b_near, b_two, b_rest = near * 4 + own, two * 4 + own, rest * 4 + own
     c_near, c_two, c_rest = near * 4 + mate, two * 4 + mate, rest * 4 + mate
@@ -530,12 +545,12 @@
             go(b_two, ch, rest * 4 + mate)
 
         go(b_two, ch, other_x)
-        beside(b_two, ch, 3 - ends)
+        beside(b_two, ch, 1 + ends)
 
     def either(at_middle, at_end):
         return (at_middle + ends * (at_end - at_middle)) // 2
 
-    attend(0, [me // 2], start=True)
+    project(0, 0, [me // 2])
     take(other_x, 0, 1)
 
     @pl.when(edge)
@@ -550,40 +565,39 @@
 
     take_two(0)
     take_two(1)
+    project(1, 1, [other_x // 2, either(b_two, b_near)])
 
     @pl.when(middle)
     def _():
         for ch in range(chunks):
-            take(c_near, ch, 1)
-            take(c_rest, ch, 2)
+            take(c_near, ch, 2)
+            take(c_rest, ch, 3)
         for ch in range(chunks):
-            take(b_rest, ch, 3)
-            take(b_near, ch, 2)
-
-    attend(1, [other_x // 2, either(c_near, b_near)])
+            take(b_rest, ch, 4)
+            take(b_near, ch, 3)
+
+    project(2, 3, [either(c_near, b_two)])
+    attend((0, 4), False)
 
     @pl.when(edge)
     def _():
-        take(c_near, 0, 2)
-        take(c_near, 1, 2)
-        take(b_rest, 0, 3)
-
-    take(c_two, 0, 4 - ends)
-    take(c_two, 1, 4 - ends)
-
-    @pl.when(edge)
-    def _():
-        take(b_rest, 1, 3)
-
-    attend(2, [either(c_rest, b_two), either(b_near, c_near)])
-
-    @pl.when(edge)
-    def _():
+        take(c_near, 0, 3)
+        take(c_near, 1, 3)
+        take(b_rest, 0, 4)
+        take(c_two, 0, 3)
+        take(c_two, 1, 3)
+        take(b_rest, 1, 4)
         take(c_rest, 0, 4)
         take(c_rest, 1, 4)
 
-    attend(3, [b_rest // 2, either(b_two, c_two)])
-    attend(4, [either(c_two, c_rest)], end=True)
+    @pl.when(middle)
+    def _():
+        take(c_two, 0, 4)
+        take(c_two, 1, 4)
+
+    project(3, 4, [either(c_rest, c_near), either(b_near, c_two)])
+    project(4, 6, [b_rest // 2, either(c_two, c_rest)])
+    attend((4, 8), True)
 
     loads[5].wait()
     final = tokens + jnp.dot(att[...], wo[...], preferred_element_type=jnp.float32)
@@ -644,6 +658,8 @@
             pltpu.VMEM((2, 2, srows, chans), bf16),
             pltpu.VMEM((2, 2, srows, chans), bf16),
             pltpu.VMEM((n, CHUNKS, toks // CHUNKS, chans), bf16),
+            pltpu.VMEM((n * toks, width), bf16),
+            pltpu.VMEM((n * toks, width), bf16),
             pltpu.VMEM((toks, width), f32),
             pltpu.VMEM((toks, width), f32),
             pltpu.VMEM((toks, width), f32),
@@ -651,6 +667,7 @@
             pltpu.VMEM((toks, width), bf16),
             pltpu.SemaphoreType.DMA((6,)),
             pltpu.SemaphoreType.REGULAR,
+            pltpu.SemaphoreType.REGULAR((3, 2)),
             pltpu.SemaphoreType.DMA((2,)),
             pltpu.SemaphoreType.DMA((5,)),
             pltpu.SemaphoreType.DMA,

time: 28 us -> 25.9 us (0.925)
  Pallas kernels: 27.2 us -> 25.1 us
    pallas_call x1, Pallas kernels: 27.2 us -> 25.1 us  [fast_body(): pl.pallas_call(functools.partial(fused_kernel, n, cols, toks, heads, HEAD...]
where the time goes in v3:
time: 25.9 us; the launch traced here: 25.8 us
  Pallas kernels  25.1 us (97%)
  local copies, waits for them, and re-layouts  0.7 us (3%)
    pallas_call x1, Pallas kernels, fast_body(): pl.pallas_call(functools.partial(fused_kernel, n, cols, toks, heads, HEAD...  25.1 us
    transpose x1, local copies, waits for them, and re-layouts, fast_body(): return out.transpose(1, 0, 2)  0.7 us

profile of v3, /device:TPU:0, one launch (start us, length us, event | category | flops | bytes accessed | tf_op | source)
XLA Modules:
  0.0 25.8 jit_solution(10383716990339270054)
XLA Ops:
  0.0 25.1 %shard_map.64 = bf16[2,32,512]{2,1,0:T(8,128)(2,1)S(1)} custom-call(bf16[1024,256]{1,0:T(8,128)(2,1)} %bitcast.8, bf16[2304,512]{1,0:T(8,128)(2,1)} %bitcast.7, bf16[4608,512]{1,0:T(8,128)(2,1)} %bitcast.6, f32[1,512]{1,0:T(1,128)} %bitcast.9, bf16[512,3072]{1,0:T(8,128)(2,1)} %wqkv_hbm.1, bf16[1024,512]{1,0:T(8,128)(2,1)} %wo_hbm.1), custom_call_target="tpu_custom_call" | custom-call | tf_op jit(solution)/shard_map/pallas_call | solution.py:643
  25.1 0.7 %copy.7 = bf16[32,2,512]{2,1,0:T(2,128)(2,1)} copy(bf16[32,2,512]{2,0,1:T(8,128)(2,1)S(1)} %bitcast.5) | data formatting | bytes 131072 | tf_op jit(solution)/shard_map/transpose | solution.py:693

commit v4 on v3

--- a/solution.py
+++ b/solution.py
@@ -139,7 +139,7 @@
     n, cols, toks, heads, hdim,
     x_hbm, wa_hbm, wb_hbm, gain_hbm, wqkv_hbm, wo_hbm, out_ref,
     x_v, wa, wb, wqkv, wo, gain_ref, xs, edge_in, ps, pedge_out, pedge_in,
-    gat, keys, vals, sums, totals, peaks, qmask, att,
+    gat, keys, vals, sums, totals, peaks, qmask,
     load_sem, near_ok, told, halo_send, halo_recv, block_send, block_recv, side_recv,
 ):
     width = heads * hdim
@@ -472,8 +472,8 @@
             got = jnp.where(heads_at == a, v[a * toks : (a + 1) * toks], got)
         return got
 
-    def project(unit, slot, chips):
-        both = gat.at[pl.ds(0, len(chips))]
+    def side(unit, count):
+        both = gat.at[pl.ds(0, count)]
         pltpu.make_async_remote_copy(
             src_ref=both,
             dst_ref=both,
@@ -481,51 +481,69 @@
             recv_sem=side_recv.at[unit],
             device_id={"lon": other_core},
         ).wait_recv()
-        have = jnp.concatenate(
+
+    def gathered(chips):
+        return jnp.concatenate(
             [gat[pl.ds(2 * c, 2)].reshape(2 * toks, chans) for c in chips], axis=0
         )
+
+    def project(unit, slot, chips):
+        side(unit, len(chips))
+        have = gathered(chips)
         made = jnp.dot(have, wqkv[:, width:], preferred_element_type=jnp.float32)
         made = made.astype(jnp.bfloat16)
         at = slice(slot * 2 * toks, (slot + len(chips)) * 2 * toks)
         keys[at] = made[:, 0:width]
         vals[at] = made[:, width:]
 
-    def attend(slots, end):
-        at = slice(slots[0] * 2 * toks, slots[1] * 2 * toks)
-        mixes, norms = {}, {}
+    def attend(made, done):
+        held, ahead = {}, {}
 
         def score(g):
             lanes = slice(g * group, (g + 1) * group)
+            these, those = ahead.pop(g)
             scores = lax.dot_general(
                 qmask[:, lanes],
-                keys[at, lanes],
+                these,
                 (((1,), (1,)), ((), ())),
                 preferred_element_type=jnp.float32,
             )
             peak = jnp.max(scores, axis=-1, keepdims=True)
             raised = jnp.exp(scores - peak)
-            norms[g] = peak, jnp.sum(raised, axis=-1, keepdims=True)
-            mixes[g] = raised.astype(jnp.bfloat16)
+            total = jnp.sum(raised, axis=-1, keepdims=True)
+            held[g] = raised.astype(jnp.bfloat16), those, peak, total
 
         def mix(g):
-            lanes = slice(g * group, (g + 1) * group)
-            mixed = jnp.dot(mixes[g], vals[at, lanes], preferred_element_type=jnp.float32)
-            got, peak, total = by_head(mixed), by_head(norms[g][0]), by_head(norms[g][1])
-            if end:
-                top = jnp.maximum(peaks[:, lanes], peak)
-                was, now = jnp.exp(peaks[:, lanes] - top), jnp.exp(peak - top)
-                got = sums[:, lanes] * was + got * now
-                total = totals[:, lanes] * was + total * now
-                att[:, lanes] = (got * (1.0 / total)).astype(jnp.bfloat16)
-            else:
-                sums[:, lanes], totals[:, lanes], peaks[:, lanes] = got, total, peak
+            raised, those, peak, total = held.pop(g)
+            mixed = jnp.dot(raised, those, preferred_element_type=jnp.float32)
+            done(g, by_head(mixed), by_head(peak), by_head(total))
 
         groups = heads // 4
+        ahead[0] = made(0)
         for step in range(groups + 1):
+            if step + 1 < groups:
+                ahead[step + 1] = made(step + 1)
             if step < groups:
                 score(step)
             if step > 0:
                 mix(step - 1)
+
+    def stored(g):
+        lanes = slice(g * group, (g + 1) * group)
+        return keys[:, lanes], vals[:, lanes]
+
+    def keep(g, got, peak, total):
+        lanes = slice(g * group, (g + 1) * group)
+        sums[:, lanes], totals[:, lanes], peaks[:, lanes] = got, total, peak
+
+    def finish(g, got, peak, total):
+        lanes = slice(g * group, (g + 1) * group)
+        top = jnp.maximum(peaks[:, lanes], peak)
+        was, now = jnp.exp(peaks[:, lanes] - top), jnp.exp(peak - top)
+        got = sums[:, lanes] * was + got * now
+        total = totals[:, lanes] * was + total * now
+        att = (got * (1.0 / total)).astype(jnp.bfloat16)
+        parts.append(jnp.dot(att, wo[lanes, :], preferred_element_type=jnp.float32))
 
     b_near, b_two, b_rest = near * 4 + own, two * 4 + own, rest * 4 + own
     c_near, c_two, c_rest = near * 4 + mate, two * 4 + mate, rest * 4 + mate
@@ -577,7 +595,7 @@
             take(b_near, ch, 3)
 
     project(2, 3, [either(c_near, b_two)])
-    attend((0, 4), False)
+    attend(stored, keep)
 
     @pl.when(edge)
     def _():
@@ -595,12 +613,29 @@
         take(c_two, 0, 4)
         take(c_two, 1, 4)
 
-    project(3, 4, [either(c_rest, c_near), either(b_near, c_two)])
-    project(4, 6, [b_rest // 2, either(c_two, c_rest)])
-    attend((4, 8), True)
-
     loads[5].wait()
-    final = tokens + jnp.dot(att[...], wo[...], preferred_element_type=jnp.float32)
+    side(3, 2)
+    side(4, 2)
+    have = gathered(
+        [
+            either(c_rest, c_near), either(b_near, c_two),
+            b_rest // 2, either(c_two, c_rest),
+        ]
+    )
+
+    def fresh(g):
+        return [
+            jnp.dot(
+                have,
+                wqkv[:, at + g * group : at + (g + 1) * group],
+                preferred_element_type=jnp.float32,
+            ).astype(jnp.bfloat16)
+            for at in (width, 2 * width)
+        ]
+
+    parts = []
+    attend(fresh, finish)
+    final = tokens + sum(parts)
     out_ref[...] = final.reshape(out_ref.shape).astype(jnp.bfloat16)
 
     def drain(ref, sem):
@@ -658,13 +693,12 @@
             pltpu.VMEM((2, 2, srows, chans), bf16),
             pltpu.VMEM((2, 2, srows, chans), bf16),
             pltpu.VMEM((n, CHUNKS, toks // CHUNKS, chans), bf16),
-            pltpu.VMEM((n * toks, width), bf16),
-            pltpu.VMEM((n * toks, width), bf16),
+            pltpu.VMEM((n // 2 * toks, width), bf16),
+            pltpu.VMEM((n // 2 * toks, width), bf16),
             pltpu.VMEM((toks, width), f32),
             pltpu.VMEM((toks, width), f32),
             pltpu.VMEM((toks, width), f32),
             pltpu.VMEM((4 * toks, width), bf16),
-            pltpu.VMEM((toks, width), bf16),
             pltpu.SemaphoreType.DMA((6,)),
             pltpu.SemaphoreType.REGULAR,
             pltpu.SemaphoreType.REGULAR((3, 2)),

time: 25.9 us -> 25.9 us (level)
  no operation moved by 1% of the time
where the time goes in v4:
time: 25.9 us; the launch traced here: 25.7 us
  Pallas kernels  25 us (97%)
  local copies, waits for them, and re-layouts  0.7 us (3%)
    pallas_call x1, Pallas kernels, fast_body(): pl.pallas_call(functools.partial(fused_kernel, n, cols, toks, heads, HEAD...  25 us
    transpose x1, local copies, waits for them, and re-layouts, fast_body(): return out.transpose(1, 0, 2)  0.7 us

profile of v4, /device:TPU:0, one launch (start us, length us, event | category | flops | bytes accessed | tf_op | source)
XLA Modules:
  0.0 25.7 jit_solution(15199443961568569918)
XLA Ops:
  0.0 25.0 %shard_map.64 = bf16[2,32,512]{2,1,0:T(8,128)(2,1)S(1)} custom-call(bf16[1024,256]{1,0:T(8,128)(2,1)} %bitcast.8, bf16[2304,512]{1,0:T(8,128)(2,1)} %bitcast.7, bf16[4608,512]{1,0:T(8,128)(2,1)} %bitcast.6, f32[1,512]{1,0:T(1,128)} %bitcast.9, bf16[512,3072]{1,0:T(8,128)(2,1)} %wqkv_hbm.1, bf16[1024,512]{1,0:T(8,128)(2,1)} %wo_hbm.1), custom_call_target="tpu_custom_call" | custom-call | tf_op jit(solution)/shard_map/pallas_call | solution.py:678
  25.0 0.7 %copy.7 = bf16[32,2,512]{2,1,0:T(2,128)(2,1)} copy(bf16[32,2,512]{2,0,1:T(8,128)(2,1)S(1)} %bitcast.5) | data formatting | bytes 131072 | tf_op jit(solution)/shard_map/transpose | solution.py:727

commit v5 on v4

--- a/solution.py
+++ b/solution.py
@@ -312,12 +312,13 @@
     jp_third = jp_far + wraps * (2 - jp_far)
     jp_fourth = 2 + jp_far - jp_third
     loads[1].wait()
+    (inside,) = conv_first(1)
+    put_pooled(2, *inside)
     by_near.wait_recv()
     put_column(3, (1 - core) * (cols + 1) + 2)
-    inside, beside_near = conv_first(1, jp_near)
+    (beside_near,) = conv_first(jp_near)
     put_pooled(jp_near + 1, *beside_near)
     put_edge(0, *beside_near)
-    put_pooled(2, *inside)
     by_near_2.start()
 
     hear(0)

time: 25.9 us -> 25.9 us (level)
  no operation moved by 1% of the time
where the time goes in v5:
time: 25.9 us; the launch traced here: 25.7 us
  Pallas kernels  25 us (97%)
  local copies, waits for them, and re-layouts  0.7 us (3%)
    pallas_call x1, Pallas kernels, fast_body(): pl.pallas_call(functools.partial(fused_kernel, n, cols, toks, heads, HEAD...  25 us
    transpose x1, local copies, waits for them, and re-layouts, fast_body(): return out.transpose(1, 0, 2)  0.7 us

profile of v5, /device:TPU:0, one launch (start us, length us, event | category | flops | bytes accessed | tf_op | source)
XLA Modules:
  0.0 25.7 jit_solution(2589219798852455238)
XLA Ops:
  0.0 25.0 %shard_map.64 = bf16[2,32,512]{2,1,0:T(8,128)(2,1)S(1)} custom-call(bf16[1024,256]{1,0:T(8,128)(2,1)} %bitcast.8, bf16[2304,512]{1,0:T(8,128)(2,1)} %bitcast.7, bf16[4608,512]{1,0:T(8,128)(2,1)} %bitcast.6, f32[1,512]{1,0:T(1,128)} %bitcast.9, bf16[512,3072]{1,0:T(8,128)(2,1)} %wqkv_hbm.1, bf16[1024,512]{1,0:T(8,128)(2,1)} %wo_hbm.1), custom_call_target="tpu_custom_call" | custom-call | tf_op jit(solution)/shard_map/pallas_call | solution.py:679
  25.0 0.7 %copy.7 = bf16[32,2,512]{2,1,0:T(2,128)(2,1)} copy(bf16[32,2,512]{2,0,1:T(8,128)(2,1)S(1)} %bitcast.5) | data formatting | bytes 131072 | tf_op jit(solution)/shard_map/transpose | solution.py:728
